TPU v7x, 32 devices: a whole 2x2x4 slice. The times are simulated.
32 devices in a mesh: dp: 8 (over z, core), tp: 4 (over y, x).
Axes of the slice: x: 2, y: 2, z: 4, core: 2. Of those that a mesh axis runs over, the one named last changes fastest.
Arguments:
- master: float32 [4096, 10240], P(('dp', 'tp')), may hold values from -0.09375 to 0.09375
- grad: float32 [4096, 10240], P(('dp', 'tp')), may hold values from -0.006 to 0.006
- exp_avg: float32 [4096, 10240], P(('dp', 'tp')), may hold values from -0.006 to 0.006
- exp_avg_sq: float32 [4096, 10240], P(('dp', 'tp')), may hold values from 1e-08 to 1e-05
Outputs:
- new_master: float32 [4096, 10240], P(('dp', 'tp'))
- new_avg: float32 [4096, 10240], P(('dp', 'tp'))
- new_avg_sq: float32 [4096, 10240], P(('dp', 'tp'))
- engine_qkv: bfloat16 [4096, 10240], P(None, 'tp')
All inputs are finite; a program needn't handle non-finite values.
Results may differ from a plain program's by a relative error of at most 0.001.
Values may be sent and summed in bfloat16 or wider, within the bound.
A program may use at most 128 MiB of HBM per device.

v0:
```python
import jax
import jax.numpy as jnp
from jax import lax
from jax.sharding import PartitionSpec as P

QH = 64
KVH = 8
HS = 128


def joined_slices(weights, tp_count):
    rows = weights.shape[0]
    query = weights[:, : QH * HS].reshape(rows, tp_count, QH // tp_count * HS)
    keys = weights[:, QH * HS : (QH + KVH) * HS].reshape(rows, tp_count, KVH // tp_count * HS)
    values = weights[:, (QH + KVH) * HS :].reshape(rows, tp_count, KVH // tp_count * HS)
    return jnp.concatenate([query, keys, values], axis=2).reshape(rows, -1)


def body(master, grad, exp_avg, exp_avg_sq):
    corr_one = 1.0 - 0.9**10
    corr_two = 1.0 - 0.999**10
    new_avg = 0.9 * exp_avg + 0.1 * grad
    new_avg_sq = 0.999 * exp_avg_sq + 0.001 * grad * grad
    update = new_avg / corr_one / (jnp.sqrt(new_avg_sq / corr_two) + 1e-08)
    new_master = master - 0.001 * (update + 0.1 * master)
    tp_count = lax.axis_size("tp")
    ordered = joined_slices(new_master, tp_count).astype(jnp.bfloat16)
    group_rows = lax.all_to_all(ordered, "tp", split_axis=1, concat_axis=0, tiled=True)
    engine_qkv = lax.all_gather(group_rows, "dp", axis=0, tiled=True)
    return (new_master, new_avg, new_avg_sq, engine_qkv)


def solution(mesh):
    in_specs = (
        P(("dp", "tp"), None),
        P(("dp", "tp"), None),
        P(("dp", "tp"), None),
        P(("dp", "tp"), None),
    )
    out_specs = (P(("dp", "tp"), None), P(("dp", "tp"), None), P(("dp", "tp"), None), P(None, "tp"))
    return jax.shard_map(body, mesh=mesh, in_specs=in_specs, out_specs=out_specs, check_vma=False)
```

profile of v0, /device:TPU:0, one launch (start us, length us, event | category | flops | bytes accessed | tf_op | source)
XLA Modules:
  0.0 267.6 jit_solution(15748844206019149272)
XLA Ops:
  7.2 0.0 all-gather.2.cloned.1.call-start
  7.2 14.4 %fusion.1 = (bf16[128,10240]{1,0:T(8,128)(2,1)S(1)}, f32[128,10240]{1,0:T(8,128)}, f32[128,10240]{1,0:T(8,128)}, f32[128,10240]{1,0:T(8,128)}) fusion(f32[128,10240]{1,0:T(8,128)} %param.4, f32[128,10240]{1,0:T(8,128)} %param.5, f32[128,10240]{1,0:T(8,128)} %param.6, f32[128,10240]{1,0:T(8,128)} %param.7), kind=kLoop, calls=%fused_computation.8 | loop fusion | flops 20971520 | bytes 39321600 | tf_op jit(solution)/shard_map/convert.8
  21.6 0.1 slice.15
  21.8 0.1 copy.17
  22.0 0.2 pad_maximum_fusion
  22.2 36.1 %all_to_all.16 = bf16[128,4,2560]{2,0,1:T(8,128)(2,1)} all-to-all(bf16[128,4,2560]{2,0,1:T(8,128)(2,1)S(1)} %pad_maximum_fusion), channel_id=1, replica_groups=mesh['dp'=8,'tp'=4] {'tp'}, dimensions={1} | all-to-all | bytes 5242880 | tf_op jit(solution)/shard_map/all_to_all | solution.py:28
  58.3 0.0 all-gather.2.cloned.1.call-update
  58.3 185.3 %all-gather.2.cloned.1.call-done = bf16[4096,2560]{1,0:T(8,128)(2,1)} async-done(((bf16[512,2560]{1,0:T(8,128)(2,1)}), bf16[4096,2560]{1,0:T(8,128)(2,1)}) %all-gather.2.cloned.1.call-update) | async-done | bytes 20971536 | tf_op jit(solution)/shard_map/all_gather | solution.py:29
  243.6 17.1 %copy.19 = bf16[4096,2560]{1,0:T(8,128)(2,1)} copy(bf16[4096,2560]{1,0:T(8,128)(2,1)} %all-gather.2.cloned.1.call-done) | data formatting | bytes 41943040
  (2 shorter events, 0.1 us)
Async XLA Ops:
  7.2 236.5 %all-gather.2.cloned.1.call-start = ((), (), s32[]{:S(2)}) async-start(), calls=%async_computation.1 | async-start | bytes 23592960 | tf_op jit(solution)/shard_map/all_gather | solution.py:29
Sparse Core Ops, SparseCore 0:
  58.4 185.1 all-gather.1
where the time goes:
time: 268 us
  waiting for transfers between devices  185 us (69%)
  blocking collectives  36.1 us (13%)
  local copies, waits for them, and re-layouts  17.5 us (7%)
  other arithmetic  14.6 us (5%)
  between operations  14.1 us (5%)
    all_gather x1, waiting for transfers between devices, body(): engine_qkv = lax.all_gather(group_rows, 'dp', axis=0, tiled=True)  185 us
    all_to_all x1, blocking collectives, body(): lax.all_to_all(ordered, 'tp', split_axis=1, concat_axis=0, tiled=True)  36.1 us
    unnamed x1, local copies, waits for them, and re-layouts  17.1 us
    another operation x1, other arithmetic  14.4 us
  transfers between devices with their start and end apart: 1, of which 1 were waited for; matrix products, arithmetic and copies ran while one was open for 0% of the time, Pallas kernels for 0%

commit v1 on v0

--- a/solution.py
+++ b/solution.py
@@ -25,7 +25,9 @@
     new_master = master - 0.001 * (update + 0.1 * master)
     tp_count = lax.axis_size("tp")
     ordered = joined_slices(new_master, tp_count).astype(jnp.bfloat16)
-    group_rows = lax.all_to_all(ordered, "tp", split_axis=1, concat_axis=0, tiled=True)
+    cells = jnp.split(ordered, lax.axis_size("tp"), axis=1)
+    received = lax.all_to_all(jnp.stack(cells), "tp", 0, 0)
+    group_rows = jnp.concatenate(received, axis=0)
     engine_qkv = lax.all_gather(group_rows, "dp", axis=0, tiled=True)
     return (new_master, new_avg, new_avg_sq, engine_qkv)
 

time: 268 us -> 275 us (1.026)
  local copies, waits for them, and re-layouts: 17.5 us -> 23 us
    reshape x1, local copies, waits for them, and re-layouts: 0.14 us -> 3.32 us  [joined_slices(): query = weights[:, :QH * HS].reshape(rows, tp_count, QH // tp_count * HS)]
    unnamed x1 -> x2, local copies, waits for them, and re-layouts: 17.1 us -> 17.6 us
    another operation x1 -> x2, other arithmetic: 14.4 us -> 14.7 us
where the time goes in v1:
time: 275 us
  waiting for transfers between devices  185 us (67%)
  blocking collectives  36.1 us (13%)
  local copies, waits for them, and re-layouts  23 us (8%)
  other arithmetic  16.1 us (6%)
  between operations  14.1 us (5%)
    all_gather x1, waiting for transfers between devices, body(): engine_qkv = lax.all_gather(group_rows, 'dp', axis=0, tiled=True)  185 us
    all_to_all x1, blocking collectives, body(): received = lax.all_to_all(jnp.stack(cells), 'tp', 0, 0)  36.1 us
    unnamed x2, local copies, waits for them, and re-layouts  17.6 us
    another operation x1, other arithmetic  14.4 us
  transfers between devices with their start and end apart: 1, of which 1 were waited for; matrix products, arithmetic and copies ran while one was open for 0% of the time, Pallas kernels for 0%

profile of v1, /device:TPU:0, one launch (start us, length us, event | category | flops | bytes accessed | tf_op | source)
XLA Modules:
  0.0 274.7 jit_solution(9596857814882081816)
XLA Ops:
  7.2 0.0 all-gather.2.cloned.1.call-start
  7.2 14.4 %fusion.1 = (bf16[128,10240]{1,0:T(8,128)(2,1)S(1)}, f32[128,10240]{1,0:T(8,128)}, f32[128,10240]{1,0:T(8,128)}, f32[128,10240]{1,0:T(8,128)}) fusion(f32[128,10240]{1,0:T(8,128)} %param.4, f32[128,10240]{1,0:T(8,128)} %param.5, f32[128,10240]{1,0:T(8,128)} %param.6, f32[128,10240]{1,0:T(8,128)} %param.7), kind=kLoop, calls=%fused_computation.10 | loop fusion | flops 20971520 | bytes 39321600 | tf_op jit(solution)/shard_map/convert.8
  21.6 1.5 slice.15
  23.1 3.3 %reshape.25 = bf16[128,4,2048]{2,1,0:T(4,128)(2,1)S(1)} reshape(bf16[128,8192]{1,0:T(8,128)(2,1)} %slice.15) | data formatting | bytes 4194304 | tf_op jit(solution)/shard_map/reshape | solution.py:13
  26.4 0.2 reshape.26
  26.6 0.2 reshape.27
  26.8 1.4 pad_maximum_fusion
  28.2 0.5 copy.8
  28.7 0.2 slice_bitcast_fusion.3
  28.9 0.3 pad_maximum_fusion.1
  29.2 36.1 %all_to_all.5 = bf16[4,128,2560]{2,1,0:T(8,128)(2,1)} all-to-all(bf16[4,128,2560]{2,1,0:T(8,128)(2,1)S(1)} %pad_maximum_fusion.1), channel_id=1, replica_groups=mesh['dp'=8,'tp'=4] {'tp'}, dimensions={0} | all-to-all | bytes 5242880 | tf_op jit(solution)/shard_map/all_to_all | solution.py:29
  65.3 0.0 all-gather.2.cloned.1.call-update
  65.4 185.3 %all-gather.2.cloned.1.call-done = bf16[4096,2560]{1,0:T(8,128)(2,1)} async-done(((bf16[512,2560]{1,0:T(8,128)(2,1)}), bf16[4096,2560]{1,0:T(8,128)(2,1)}) %all-gather.2.cloned.1.call-update) | async-done | bytes 20971536 | tf_op jit(solution)/shard_map/all_gather | solution.py:31
  250.7 17.1 %copy.10 = bf16[4096,2560]{1,0:T(8,128)(2,1)} copy(bf16[4096,2560]{1,0:T(8,128)(2,1)} %all-gather.2.cloned.1.call-done) | data formatting | bytes 41943040
  (1 shorter events, 0.0 us)
Async XLA Ops:
  7.2 243.5 %all-gather.2.cloned.1.call-start = ((), (), s32[]{:S(2)}) async-start(), calls=%async_computation.1 | async-start | bytes 23592960 | tf_op jit(solution)/shard_map/all_gather | solution.py:31
Sparse Core Ops, SparseCore 0:
  65.5 185.1 all-gather.1
